TPU v7x, 512 devices: a whole 4x4x16 slice. The times are simulated.
512 devices in a mesh: row: 16 (over x, y), col: 32 (over z, core).
Axes of the slice: x: 4, y: 4, z: 16, core: 2. Of those that a mesh axis runs over, the one named last changes fastest.
Arguments:
- start_vector: bfloat16 [4, 2048, 2048], P(None, 'row', 'col'), may hold values from -150 to 150
- left_env: bfloat16 [5, 2048, 2048], P(None, 'row', 'col'), may hold values from -5 to 6
- right_env: bfloat16 [5, 2048, 2048], P(None, 'col', 'row'), may hold values from -5 to 6
- left_tensor: float32 [5, 5, 2, 2], replicated, may hold values from -1.5 to 2.5
- right_tensor: float32 [5, 5, 2, 2], replicated, may hold values from -1.5 to 2.5
Outputs:
- next_vector: bfloat16 [4, 2048, 2048], P(None, 'row', 'col')
- coefficients: float32 [2], replicated
All inputs are finite; a program needn't handle non-finite values.
Results may differ from a plain program's by a relative error of at most 0.023.
Values may be sent and summed in bfloat16 or wider, within the bound.
No kernel may reach another device: no remote copies, remote signals or barrier semaphores. Data moves between devices by JAX's collectives and lax.ppermute only.
A program may use at most 64 MiB of HBM per device.

v0:
```python
import jax
import jax.numpy as jnp
from jax import lax
from jax.sharding import Mesh
from jax.sharding import PartitionSpec as P

ROW = ("row_0", "row_1")
COL = ("col_0", "col_1")
ROW_COL = ("row_0", "row_1", "col_0", "col_1")
epsilon = 1e-06


def copy_for_each(x, axis):
    size = lax.axis_size(axis)
    return lax.all_to_all(jnp.broadcast_to(x[None], (size, *x.shape)), axis, 0, 0, tiled=True)


def joined_along(pieces, dim):
    pieces = jnp.moveaxis(pieces, 0, dim)
    lengths = pieces.shape
    return pieces.reshape(*lengths[:dim], lengths[dim] * lengths[dim + 1], *lengths[dim + 2 :])


def gathered_copies(x, axis, dim):
    pieces = copy_for_each(x, axis)
    return joined_along(pieces, dim)


def sum_in_order(pieces, axes, sequence):
    lengths = [lax.axis_size(a) for a in axes]
    pieces = pieces.reshape(*lengths, *pieces.shape[1:])
    pieces = pieces.transpose(*sequence, *range(len(axes), pieces.ndim))
    pieces = pieces.reshape(-1, *pieces.shape[len(axes) :])
    for k in sequence:
        pieces = lax.psum_scatter(pieces, axes[k], scatter_dimension=0, tiled=True)
    return pieces[0]


def cut_along(x, dim, size):
    lengths = x.shape
    pieces = x.reshape(*lengths[:dim], size, lengths[dim] // size, *lengths[dim + 1 :])
    return jnp.moveaxis(pieces, dim, 0)


def scatter_axes(x, axes, sequence, dim):
    size = lax.axis_size(axes)
    return sum_in_order(cut_along(x, dim, size), axes, sequence)


def by_axis(x, axes):
    for axis in axes:
        x = lax.psum(x, axis)
    return x


def coupling(left_tensor, right_tensor):
    channels = left_tensor.shape[0]
    joined = jnp.einsum(
        "wuac,uvbd->vabwcd", left_tensor, right_tensor, precision=lax.Precision.HIGHEST
    )
    return joined.reshape(channels, 4, channels, 4)


def contract_left(portion, columns):
    return jnp.einsum("wax,txb->wtba", portion, columns, preferred_element_type=jnp.float32)


def mix_channels(coupling_table, cross):
    mixed_bond = jnp.einsum(
        "vswt,wtba->vsba", coupling_table, cross, precision=lax.Precision.HIGHEST
    )
    return mixed_bond.astype(jnp.bfloat16)


def contract_right(mixed_bond, portion):
    return jnp.einsum("vsba,vbc->sac", mixed_bond, portion, preferred_element_type=jnp.float32)


def apply_hamiltonian(vector, coupling_table, panels):
    columns = gathered_copies(vector, ROW, 1)
    cross = contract_left(panels[0], columns)
    mixed_bond = mix_channels(coupling_table, cross)
    partials = contract_right(mixed_bond, panels[1])
    return scatter_axes(partials.astype(jnp.bfloat16), COL, (1, 0), 2).astype(jnp.float32)


def local_mean(former, latter, entries):
    return jnp.sum(former * latter) / entries


def body(start_vector, left_env, right_env, left_tensor, right_tensor):
    coupling_table = coupling(left_tensor, right_tensor)
    entries = float(
        start_vector.shape[0]
        * start_vector.shape[1]
        * start_vector.shape[2]
        * lax.axis_size(ROW)
        * lax.axis_size(COL)
    )
    panels = (lax.all_gather(left_env, COL, axis=2, tiled=True), gathered_copies(right_env, ROW, 2))
    base_vector = start_vector.astype(jnp.float32)
    image = apply_hamiltonian(start_vector, coupling_table, panels)
    base_square, correlation, image_square = (
        by_axis(local_mean(base_vector, base_vector, entries), ROW_COL),
        by_axis(local_mean(base_vector, image, entries), ROW_COL),
        by_axis(local_mean(image, image, entries), ROW_COL),
    )
    alpha = correlation / (base_square + epsilon)
    residual = image - alpha * base_vector
    rho = jnp.sqrt(image_square - 2.0 * alpha * correlation + alpha * alpha * base_square + epsilon)
    next_vector = (residual / rho).astype(jnp.bfloat16)
    coefficients = jnp.stack([alpha, rho])
    return (next_vector, coefficients)


def solution(mesh):
    finer = Mesh(mesh.devices.reshape(4, 4, 16, 2), ("row_0", "row_1", "col_0", "col_1"))
    in_specs = (P(None, ROW, COL), P(None, ROW, COL), P(None, COL, ROW), P(), P())
    out_specs = (P(None, ROW, COL), P())
    return jax.shard_map(body, mesh=finer, in_specs=in_specs, out_specs=out_specs, check_vma=False)
```

profile of v0, /device:TPU:1, one launch (start us, length us, event | category | flops | bytes accessed | tf_op | source)
XLA Modules:
  0.0 263.9 jit_solution(11655160880378192590)
XLA Ops:
  7.2 0.0 copy-start
  7.2 0.0 all-gather.2.cloned.1.call-start
  7.2 0.7 all-gather.2.cloned.1.call-update
  7.9 1.1 broadcast_in_dim.4
  9.0 22.4 %all_to_all.10 = bf16[16,4,128,64]{2,3,1,0:T(8,128)(2,1)S(1)} all-to-all(bf16[16,4,128,64]{2,3,1,0:T(8,128)(2,1)S(1)} %broadcast_in_dim.4), channel_id=1, replica_groups=mesh['row_0'=4,'row_1'=4,'col_0'=16,'col_1'=2] {'row_0','row_1'}, dimensions={0} | all-to-all | bytes 2097152 | tf_op jit(solution)/shard_map/all_to_all | solution.py:15
  31.4 1.4 broadcast_in_dim.5
  32.8 3.7 %all-to-all-start.1 = ((bf16[16,5,64,128]{3,2,1,0:T(8,128)(2,1)}), bf16[16,5,64,128]{3,2,1,0:T(8,128)(2,1)S(1)}, u32[]{:S(2)}, u32[]{:S(2)}) async-start(bf16[16,5,64,128]{3,2,1,0:T(8,128)(2,1)} %broadcast_in_dim.5), calls=%async_computation.1 | async-start | bytes 2621440 | tf_op jit(solution)/shard_map/all_to_all | solution.py:15
  36.5 0.0 reduce-scatter.3.cloned.1.call-start
  36.6 0.4 convolution_bitcast_fusion.1
  37.0 0.7 copy.19
  37.7 1.3 reshape.35
  39.0 14.3 %all-to-all-done.1 = bf16[16,5,64,128]{3,2,1,0:T(8,128)(2,1)S(1)} async-done(((bf16[16,5,64,128]{3,2,1,0:T(8,128)(2,1)}), bf16[16,5,64,128]{3,2,1,0:T(8,128)(2,1)S(1)}, u32[]{:S(2)}, u32[]{:S(2)}) %all-to-all-start.1) | async-done | bytes 1310752 | tf_op jit(solution)/shard_map/all_to_all | solution.py:15
  53.3 0.9 copy.22
  54.2 0.6 reshape.40
  54.8 33.2 %all-gather.2.cloned.1.call-done = bf16[5,128,2048]{1,2,0:T(8,128)(2,1)} async-done(((bf16[5,128,64]{1,2,0:T(8,128)(2,1)}), bf16[5,128,2048]{1,2,0:T(8,128)(2,1)}) %all-gather.2.cloned.1.call-update) | async-done | bytes 2621456 | tf_op jit(solution)/shard_map/all_gather | solution.py:100
  88.0 3.0 %fusion.3 = f32[5,4,64,128]{3,2,0,1:T(8,128)S(1)} fusion(bf16[5,128,2048]{1,2,0:T(8,128)(2,1)} %all-gather.2.cloned.1.call-done, bf16[4,2048,64,1]{1,2,0,3:T(8,128)(2,1)} %reshape.35), kind=kOutput, calls=%fused_computation.5 | convolution fusion | flops 671088640 | bytes 4325376 | tf_op jit(solution)/shard_map/wax,txb->wtba/dot_general | solution.py:65
  91.1 4.0 %fusion.2 = bf16[5,4,64,128]{3,0,2,1:T(8,128)(2,1)S(1)} fusion(f32[5,4,64,128]{3,2,0,1:T(8,128)S(1)} %fusion.3, f32[5,4,5,4,1]{2,3,1,0,4:T(4,128)S(1)} %bitcast.57), kind=kOutput, calls=%fused_computation.4 | convolution fusion | flops 39485440 | bytes 984640 | tf_op jit(solution)/shard_map/vswt,wtba->vsba/dot_general | solution.py:69
  95.1 1.3 bitcast_convert_fusion
  96.4 2.5 copy.24
  98.9 3.2 %copy.25 = bf16[2,16,4,128,64]{3,4,2,1,0:T(8,128)(2,1)} copy(bf16[2,16,4,128,64]{3,4,0,1,2:T(8,128)(2,1)} %bitcast.54) | data formatting | bytes 4194304 | tf_op jit(solution)/shard_map/transpose | solution.py:32
  102.1 0.0 reduce-scatter.3.cloned.1.call-update
  102.1 0.0 reduce-scatter.5.cloned.1.call-start
  102.1 17.6 %reduce-scatter.3.cloned.1.call-done = bf16[16,4,128,64]{2,3,1,0:T(8,128)(2,1)} async-done(((bf16[32,4,128,64]{2,3,1,0:T(8,128)(2,1)}), bf16[16,4,128,64]{2,3,1,0:T(8,128)(2,1)}) %reduce-scatter.3.cloned.1.call-update) | async-done | bytes 1048592 | tf_op jit(solution)/shard_map/reduce_scatter | solution.py:35
  119.8 0.0 reduce-scatter.5.cloned.1.call-update
  119.8 64.3 %reduce-scatter.5.cloned.1.call-done = bf16[1,4,128,64]{2,3,1,0:T(8,128)(2,1)} async-done(((bf16[16,4,128,64]{2,3,1,0:T(8,128)(2,1)}), bf16[1,4,128,64]{2,3,1,0:T(8,128)(2,1)}) %reduce-scatter.5.cloned.1.call-update) | async-done | bytes 65552 | tf_op jit(solution)/shard_map/reduce_scatter | solution.py:35
  184.0 1.5 fusion.10
  187.5 9.5 %all-reduce.2 = (f32[]{:T(128)}, f32[]{:T(128)}, f32[]{:T(128)}) all-reduce(f32[]{:T(128)S(6)} %div.21, f32[]{:T(128)S(6)} %div.18, f32[]{:T(128)S(6)} %div.19), channel_id=1, replica_groups=mesh['row_0'=4,'row_1'=4,'col_0'=16,'col_1'=2] {'row_0'}, use_global_device_ids=true, to_apply=%region_13.0 | all-reduce | flops 3 | bytes 24 | tf_op jit(solution)/shard_map/psum | solution.py:52
  196.9 8.5 %all-reduce.1 = (f32[]{:T(128)}, f32[]{:T(128)}, f32[]{:T(128)}) all-reduce(f32[]{:T(128)} %get-tuple-element.11, f32[]{:T(128)} %get-tuple-element.12, f32[]{:T(128)} %get-tuple-element.13), channel_id=1, replica_groups=mesh['row_0'=4,'row_1'=4,'col_0'=16,'col_1'=2] {'row_1'}, use_global_device_ids=true, to_apply=%region_14.0 | all-reduce | flops 3 | bytes 24 | tf_op jit(solution)/shard_map/psum | solution.py:52
  205.5 22.2 %all-reduce = (f32[]{:T(128)}, f32[]{:T(128)}, f32[]{:T(128)}) all-reduce(f32[]{:T(128)} %get-tuple-element.8, f32[]{:T(128)} %get-tuple-element.9, f32[]{:T(128)} %get-tuple-element.10), channel_id=1, replica_groups=mesh['row_0'=4,'row_1'=4,'col_0'=16,'col_1'=2] {'col_0'}, use_global_device_ids=true, to_apply=%region_15.0 | all-reduce | flops 3 | bytes 24 | tf_op jit(solution)/shard_map/psum | solution.py:52
  227.7 24.4 %all-reduce.3 = (f32[]{:T(128)}, f32[]{:T(128)}, f32[]{:T(128)}) all-reduce(f32[]{:T(128)} %get-tuple-element.5, f32[]{:T(128)} %get-tuple-element.6, f32[]{:T(128)} %get-tuple-element.7), channel_id=1, replica_groups=mesh['row_0'=4,'row_1'=4,'col_0'=16,'col_1'=2] {'col_1'}, use_global_device_ids=true, to_apply=%region_16.0 | all-reduce | flops 3 | bytes 24 | tf_op jit(solution)/shard_map/psum | solution.py:52
  255.3 0.6 pad_maximum_fusion
  255.8 1.5 fusion.13
  (8 shorter events, 0.0 us)
Async XLA Ops:
  7.2 29.4 %copy-start = (f32[5,5,2,2]{1,3,2,0:T(2,128)S(1)}, f32[5,5,2,2]{1,3,2,0:T(2,128)}, u32[]{:S(2)}) copy-start(f32[5,5,2,2]{1,3,2,0:T(2,128)} %param.8) | copy-start | bytes 1204
  7.2 24.2 %copy-start.2 = (bf16[5,64,128]{2,1,0:T(8,128)(2,1)S(1)}, bf16[5,64,128]{2,1,0:T(8,128)(2,1)}, u32[]{:S(2)}) copy-start(bf16[5,64,128]{2,1,0:T(8,128)(2,1)} %param.7) | copy-start | bytes 245764
  7.2 80.8 %all-gather.2.cloned.1.call-start = ((), (), s32[]{:S(2)}) async-start(), calls=%async_computation.4 | async-start | bytes 2703360 | tf_op jit(solution)/shard_map/all_gather | solution.py:100
  31.4 5.2 %copy-start.3 = (f32[5,5,2,2]{1,3,2,0:T(2,128)S(1)}, f32[5,5,2,2]{1,3,2,0:T(2,128)}, u32[]{:S(2)}) copy-start(f32[5,5,2,2]{1,3,2,0:T(2,128)} %param.9) | copy-start | bytes 1204
  32.8 20.5 %all-to-all-start.1 = ((bf16[16,5,64,128]{3,2,1,0:T(8,128)(2,1)}), bf16[16,5,64,128]{3,2,1,0:T(8,128)(2,1)S(1)}, u32[]{:S(2)}, u32[]{:S(2)}) async-start(bf16[16,5,64,128]{3,2,1,0:T(8,128)(2,1)} %broadcast_in_dim.5), calls=%async_computation.1 | async-start | bytes 2621440 | tf_op jit(solution)/shard_map/all_to_all | solution.py:15
  36.5 83.2 %reduce-scatter.3.cloned.1.call-start = ((), (), s32[]{:S(2)}) async-start(), calls=%async_computation.5 | async-start | bytes 3145728 | tf_op jit(solution)/shard_map/reduce_scatter | solution.py:35
  102.1 82.0 %copy-start.1 = (bf16[4,128,64]{1,2,0:T(8,128)(2,1)S(1)}, bf16[4,128,64]{1,2,0:T(8,128)(2,1)}, u32[]{:S(2)}) copy-start(bf16[4,128,64]{1,2,0:T(8,128)(2,1)} %param.5) | copy-start | bytes 196612
  102.1 82.0 %reduce-scatter.5.cloned.1.call-start = ((), (), s32[]{:S(2)}) async-start(), calls=%async_computation.6 | async-start | bytes 1114112 | tf_op jit(solution)/shard_map/reduce_scatter | solution.py:35
Sparse Core Ops, SparseCore 0:
  10.1 77.8 all-gather.1
  102.2 17.5 reduce-scatter.2
  122.6 61.4 reduce-scatter.4
where the time goes:
time: 264 us
  waiting for transfers between devices  130 us (49%)
  blocking collectives  87.1 us (33%)
  between operations  18.9 us (7%)
  local copies, waits for them, and re-layouts  11.7 us (4%)
  matrix products  8.74 us (3%)
  starting transfers between devices  3.82 us (1%)
  other arithmetic  3.6 us (1%)
    reduce_scatter x2, waiting for transfers between devices, sum_in_order(): pieces = lax.psum_scatter(pieces, axes[k], scatter_dimension=0, tiled=True)  81.9 us
    psum x4, blocking collectives, by_axis(): x = lax.psum(x, axis)  64.7 us
    all_gather x1, waiting for transfers between devices, body(): lax.all_gather(left_env, COL, axis=2, tiled=True)  33.2 us
    all_to_all x1, blocking collectives, copy_for_each(): lax.all_to_all(jnp.broadcast_to(x[None], (size, *x.shape)), axis, 0, 0, t...  22.4 us
    all_to_all x1, waiting for transfers between devices, copy_for_each(): lax.all_to_all(jnp.broadcast_to(x[None], (size, *x.shape)), axis, 0, 0, t...  14.3 us
  transfers between devices with their start and end apart: 4, of which 4 were waited for; matrix products, arithmetic and copies ran while one was open for 2% of the time, Pallas kernels for 0%

commit v1 on v0

--- a/solution.py
+++ b/solution.py
@@ -97,7 +97,12 @@
         * lax.axis_size(ROW)
         * lax.axis_size(COL)
     )
-    panels = (lax.all_gather(left_env, COL, axis=2, tiled=True), gathered_copies(right_env, ROW, 2))
+    panels = (
+        jnp.concatenate(
+            lax.all_to_all(jnp.stack([left_env] * lax.axis_size(COL)), COL, 0, 0), axis=2
+        ),
+        gathered_copies(right_env, ROW, 2),
+    )
     base_vector = start_vector.astype(jnp.float32)
     image = apply_hamiltonian(start_vector, coupling_table, panels)
     base_square, correlation, image_square = (

time: 264 us -> 365 us (1.38)
  waiting for transfers between devices: 130 us -> 185 us
  blocking collectives: 87.1 us -> 106 us
  starting transfers between devices: 3.82 us -> 21.6 us
  local copies, waits for them, and re-layouts: 11.7 us -> 22.3 us
    all_to_all x1, waiting for transfers between devices: 14.3 us -> 107 us  [body(): lax.all_to_all(jnp.stack([left_env] * lax.axis_size(COL)), COL, 0, 0)]
    all_gather x1 -> x0, waiting for transfers between devices: 33.2 us -> none  [body(): lax.all_gather(left_env, COL, axis=2, tiled=True)]
    all_to_all x1 -> x2, blocking collectives: 22.4 us -> 41.5 us  [copy_for_each(): lax.all_to_all(jnp.broadcast_to(x[None], (size, *x.shape)), axis, 0, 0, t...]
    all_to_all x1, starting transfers between devices: 3.7 us -> 21.6 us  [body(): lax.all_to_all(jnp.stack([left_env] * lax.axis_size(COL)), COL, 0, 0)]
    transpose x2, local copies, waits for them, and re-layouts: 1.53 us -> 6.16 us  [joined_along(): pieces = jnp.moveaxis(pieces, 0, dim)]
    reduce_scatter x2, waiting for transfers between devices: 81.9 us -> 77.7 us  [sum_in_order(): pieces = lax.psum_scatter(pieces, axes[k], scatter_dimension=0, tiled=True)]
    reshape x2, local copies, waits for them, and re-layouts: 1.88 us -> 5.53 us  [joined_along(): pieces.reshape(*lengths[:dim], lengths[dim] * lengths[dim + 1], *lengths[...]
  transfers between devices with their start and end apart: 4 -> 3, of which waited for: 4 -> 3; matrix products, arithmetic and copies ran while one was open for 2% -> 3% of each run, Pallas kernels for 0% -> 0%
where the time goes in v1:
time: 365 us; the launch traced here: 364 us
  waiting for transfers between devices  185 us (51%)
  blocking collectives  106 us (29%)
  local copies, waits for them, and re-layouts  22.3 us (6%)
  starting transfers between devices  21.6 us (6%)
  between operations  19.2 us (5%)
  matrix products  6.67 us (2%)
    all_to_all x1, waiting for transfers between devices, body(): lax.all_to_all(jnp.stack([left_env] * lax.axis_size(COL)), COL, 0, 0)  107 us
    reduce_scatter x2, waiting for transfers between devices, sum_in_order(): pieces = lax.psum_scatter(pieces, axes[k], scatter_dimension=0, tiled=True)  77.7 us
    psum x4, blocking collectives, by_axis(): x = lax.psum(x, axis)  64.5 us
    all_to_all x2, blocking collectives, copy_for_each(): lax.all_to_all(jnp.broadcast_to(x[None], (size, *x.shape)), axis, 0, 0, t...  41.5 us
    all_to_all x1, starting transfers between devices, body(): lax.all_to_all(jnp.stack([left_env] * lax.axis_size(COL)), COL, 0, 0)  21.6 us
  transfers between devices with their start and end apart: 3, of which 3 were waited for; matrix products, arithmetic and copies ran while one was open for 3% of the time, Pallas kernels for 0%

profile of v1, /device:TPU:1, one launch (start us, length us, event | category | flops | bytes accessed | tf_op | source)
XLA Modules:
  0.0 364.2 jit_solution(14813103531423550207)
XLA Ops:
  7.2 1.1 broadcast_in_dim.4
  8.3 21.9 %all_to_all.15 = bf16[16,4,128,64]{2,3,1,0:T(8,128)(2,1)} all-to-all(bf16[16,4,128,64]{2,3,1,0:T(8,128)(2,1)S(1)} %broadcast_in_dim.4), channel_id=1, replica_groups=mesh['row_0'=4,'row_1'=4,'col_0'=16,'col_1'=2] {'row_0','row_1'}, dimensions={0} | all-to-all | bytes 2097152 | tf_op jit(solution)/shard_map/all_to_all | solution.py:15
  30.2 0.3 broadcast_in_dim.5
  30.5 19.6 %all_to_all.16 = bf16[16,5,64,128]{3,2,1,0:T(8,128)(2,1)} all-to-all(bf16[16,5,64,128]{3,2,1,0:T(8,128)(2,1)S(1)} %broadcast_in_dim.5), channel_id=1, replica_groups=mesh['row_0'=4,'row_1'=4,'col_0'=16,'col_1'=2] {'row_0','row_1'}, dimensions={0} | all-to-all | bytes 2621440 | tf_op jit(solution)/shard_map/all_to_all | solution.py:15
  50.1 2.2 stack.8
  52.3 21.6 %all-to-all-start.1 = ((bf16[32,5,128,64]{2,3,1,0:T(8,128)(2,1)}), bf16[32,5,128,64]{2,3,1,0:T(8,128)(2,1)S(1)}, u32[]{:S(2)}, u32[]{:S(2)}) async-start(bf16[32,5,128,64]{2,3,1,0:T(8,128)(2,1)} %stack.8), calls=%async_computation.1 | async-start | bytes 5242880 | tf_op jit(solution)/shard_map/all_to_all | solution.py:102
  73.8 0.0 reduce-scatter.3.cloned.1.call-start
  73.9 0.4 convolution_bitcast_fusion.2
  74.4 2.9 copy.20
  77.3 2.3 reshape.45
  79.6 3.3 copy.25
  82.8 3.2 reshape.50
  86.0 107.2 %all-to-all-done.1 = bf16[32,5,128,64]{2,3,1,0:T(8,128)(2,1)S(1)} async-done(((bf16[32,5,128,64]{2,3,1,0:T(8,128)(2,1)}), bf16[32,5,128,64]{2,3,1,0:T(8,128)(2,1)S(1)}, u32[]{:S(2)}, u32[]{:S(2)}) %all-to-all-start.1) | async-done | bytes 2621472 | tf_op jit(solution)/shard_map/all_to_all | solution.py:102
  193.3 0.6 copy.21
  193.8 0.7 copy-done.2
  194.5 1.0 convolution_bitcast_fusion.1
  195.5 4.0 %fusion = bf16[5,4,64,128]{3,0,2,1:T(8,128)(2,1)S(1)} fusion(f32[5,4,64,128]{3,2,0,1:T(8,128)S(1)} %convolution_bitcast_fusion.1, f32[5,4,5,4,1]{2,3,1,0,4:T(4,128)S(1)} %bitcast.59), kind=kOutput, calls=%fused_computation.2 | convolution fusion | flops 39485440 | bytes 984640 | tf_op jit(solution)/shard_map/vswt,wtba->vsba/dot_general | solution.py:69
  199.5 1.3 bitcast_convert_fusion
  200.8 2.5 copy.27
  203.3 3.2 copy.28
  206.5 0.0 reduce-scatter.3.cloned.1.call-update
  206.5 0.0 reduce-scatter.5.cloned.1.call-start
  206.5 13.2 %reduce-scatter.3.cloned.1.call-done = bf16[16,4,128,64]{2,3,1,0:T(8,128)(2,1)} async-done(((bf16[32,4,128,64]{2,3,1,0:T(8,128)(2,1)}), bf16[16,4,128,64]{2,3,1,0:T(8,128)(2,1)}) %reduce-scatter.3.cloned.1.call-update) | async-done | bytes 1048592 | tf_op jit(solution)/shard_map/reduce_scatter | solution.py:35
  219.7 0.0 reduce-scatter.5.cloned.1.call-update
  219.8 64.5 %reduce-scatter.5.cloned.1.call-done = bf16[1,4,128,64]{2,3,1,0:T(8,128)(2,1)} async-done(((bf16[16,4,128,64]{2,3,1,0:T(8,128)(2,1)}), bf16[1,4,128,64]{2,3,1,0:T(8,128)(2,1)}) %reduce-scatter.5.cloned.1.call-update) | async-done | bytes 65552 | tf_op jit(solution)/shard_map/reduce_scatter | solution.py:35
  284.2 1.5 fusion.5
  287.7 8.7 %all-reduce.2 = (f32[]{:T(128)}, f32[]{:T(128)}, f32[]{:T(128)}) all-reduce(f32[]{:T(128)S(6)} %div.21, f32[]{:T(128)S(6)} %div.18, f32[]{:T(128)S(6)} %div.19), channel_id=1, replica_groups=mesh['row_0'=4,'row_1'=4,'col_0'=16,'col_1'=2] {'row_0'}, use_global_device_ids=true, to_apply=%region_13.0 | all-reduce | flops 3 | bytes 24 | tf_op jit(solution)/shard_map/psum | solution.py:52
  296.4 9.5 %all-reduce.1 = (f32[]{:T(128)}, f32[]{:T(128)}, f32[]{:T(128)}) all-reduce(f32[]{:T(128)} %get-tuple-element.11, f32[]{:T(128)} %get-tuple-element.12, f32[]{:T(128)} %get-tuple-element.13), channel_id=1, replica_groups=mesh['row_0'=4,'row_1'=4,'col_0'=16,'col_1'=2] {'row_1'}, use_global_device_ids=true, to_apply=%region_14.0 | all-reduce | flops 3 | bytes 24 | tf_op jit(solution)/shard_map/psum | solution.py:52
  305.9 21.8 %all-reduce = (f32[]{:T(128)}, f32[]{:T(128)}, f32[]{:T(128)}) all-reduce(f32[]{:T(128)} %get-tuple-element.8, f32[]{:T(128)} %get-tuple-element.9, f32[]{:T(128)} %get-tuple-element.10), channel_id=1, replica_groups=mesh['row_0'=4,'row_1'=4,'col_0'=16,'col_1'=2] {'col_0'}, use_global_device_ids=true, to_apply=%region_15.0 | all-reduce | flops 3 | bytes 24 | tf_op jit(solution)/shard_map/psum | solution.py:52
  327.7 24.5 %all-reduce.3 = (f32[]{:T(128)}, f32[]{:T(128)}, f32[]{:T(128)}) all-reduce(f32[]{:T(128)} %get-tuple-element.5, f32[]{:T(128)} %get-tuple-element.6, f32[]{:T(128)} %get-tuple-element.7), channel_id=1, replica_groups=mesh['row_0'=4,'row_1'=4,'col_0'=16,'col_1'=2] {'col_1'}, use_global_device_ids=true, to_apply=%region_16.0 | all-reduce | flops 3 | bytes 24 | tf_op jit(solution)/shard_map/psum | solution.py:52
  355.3 0.6 pad_maximum_fusion
  355.9 1.5 fusion.8
  (14 shorter events, 0.1 us)
Async XLA Ops:
  7.2 66.7 %copy-start = (f32[5,5,2,2]{1,3,2,0:T(2,128)S(1)}, f32[5,5,2,2]{1,3,2,0:T(2,128)}, u32[]{:S(2)}) copy-start(f32[5,5,2,2]{1,3,2,0:T(2,128)} %param.8) | copy-start | bytes 1204
  7.2 23.0 %copy-start.4 = (bf16[5,64,128]{2,1,0:T(8,128)(2,1)S(1)}, bf16[5,64,128]{2,1,0:T(8,128)(2,1)}, u32[]{:S(2)}) copy-start(bf16[5,64,128]{2,1,0:T(8,128)(2,1)} %param.7) | copy-start | bytes 245764
  30.2 19.9 %copy-start.5 = (bf16[5,128,64]{1,2,0:T(8,128)(2,1)S(1)}, bf16[5,128,64]{1,2,0:T(8,128)(2,1)}, u32[]{:S(2)}) copy-start(bf16[5,128,64]{1,2,0:T(8,128)(2,1)} %param.6) | copy-start | bytes 245764
  52.3 21.6 %copy-start.6 = (f32[5,5,2,2]{1,3,2,0:T(2,128)S(1)}, f32[5,5,2,2]{1,3,2,0:T(2,128)}, u32[]{:S(2)}) copy-start(f32[5,5,2,2]{1,3,2,0:T(2,128)} %param.9) | copy-start | bytes 1204
  52.3 141.0 %all-to-all-start.1 = ((bf16[32,5,128,64]{2,3,1,0:T(8,128)(2,1)}), bf16[32,5,128,64]{2,3,1,0:T(8,128)(2,1)S(1)}, u32[]{:S(2)}, u32[]{:S(2)}) async-start(bf16[32,5,128,64]{2,3,1,0:T(8,128)(2,1)} %stack.8), calls=%async_computation.1 | async-start | bytes 5242880 | tf_op jit(solution)/shard_map/all_to_all | solution.py:102
  73.8 145.9 %reduce-scatter.3.cloned.1.call-start = ((), (), s32[]{:S(2)}) async-start(), calls=%async_computation.5 | async-start | bytes 3145728 | tf_op jit(solution)/shard_map/reduce_scatter | solution.py:35
  193.3 1.2 copy-start.2
  194.5 5.0 %copy-start.1 = (bf16[5,64,2048,1]{2,1,0,3:T(8,128)(2,1)S(1)}, bf16[5,64,2048,1]{2,1,0,3:T(8,128)(2,1)}, u32[]{:S(2)}) copy-start(bf16[5,64,2048,1]{2,1,0,3:T(8,128)(2,1)} %reshape.50) | copy-start | bytes 3932164
  206.5 77.8 %copy-start.3 = (bf16[4,128,64]{1,2,0:T(8,128)(2,1)S(1)}, bf16[4,128,64]{1,2,0:T(8,128)(2,1)}, u32[]{:S(2)}) copy-start(bf16[4,128,64]{1,2,0:T(8,128)(2,1)} %param.5) | copy-start | bytes 196612
  206.5 77.7 %reduce-scatter.5.cloned.1.call-start = ((), (), s32[]{:S(2)}) async-start(), calls=%async_computation.6 | async-start | bytes 1114112 | tf_op jit(solution)/shard_map/reduce_scatter | solution.py:35
Sparse Core Ops, SparseCore 0:
  206.6 13.0 reduce-scatter.2
  222.5 61.6 reduce-scatter.4
